TPU v7x, 128 devices: a whole 4x4x4 slice. The times are simulated.
128 devices in a mesh: section: 4 (over y_hi, core), fsdp: 32 (over z, x, y_lo).
Axes of the slice: x: 4, y: 4 (y_hi: 2, y_lo: 2; y = y_hi * 2 + y_lo), z: 4, core: 2. Of those that a mesh axis runs over, the one named last changes fastest.
Arguments:
- hidden_in: bfloat16 [4096, 4096], P('fsdp'), may hold values from -6 to 6
- out_grad: bfloat16 [4096, 4096], P('fsdp'), may hold values from -6 to 6
- fast_in: float32 [4, 4096, 1024], P('section', 'fsdp'), may hold values from -6 to 6
- fast_out: float32 [4, 1024, 4096], P('section', None, 'fsdp'), may hold values from -6 to 6
- slow_in: float32 [4, 4096, 1024], P('section', 'fsdp'), may hold values from -6 to 6
- slow_out: float32 [4, 1024, 4096], P('section', None, 'fsdp'), may hold values from -6 to 6
Outputs:
- section_out: bfloat16 [4, 4096, 4096], P('section', 'fsdp')
- input_grad: bfloat16 [4, 4096, 4096], P('section', 'fsdp')
- synced_in: float32 [4, 4096, 1024], P('section', 'fsdp')
- synced_out: float32 [4, 1024, 4096], P('section', None, 'fsdp')
All inputs are finite; a program needn't handle non-finite values.
Results may differ from a plain program's by a relative error of at most 0.014.
Values may be sent and summed in bfloat16 or wider, within the bound.
A program may use at most 896 MiB of HBM per device.

v0:
```python
import math
import jax
import jax.numpy as jnp
from jax import lax
from jax.sharding import PartitionSpec as P

epsilon = 1e-05
fast_rate = 0.5
preview_mix = 0.5


def gather_turned(arrays, axis, dims):
    turned = [jnp.moveaxis(a, dim, 0) for a, dim in zip(arrays, dims)]
    widths = [t[0].size for t in turned]
    both = jnp.concatenate([t.reshape(-1, w) for t, w in zip(turned, widths)], axis=1)
    result = lax.all_gather(both, axis, axis=0, tiled=True)
    pieces = jnp.split(result, [sum(widths[:k]) for k in range(1, len(widths))], axis=1)
    return tuple(
        (
            jnp.moveaxis(b.reshape(-1, *t.shape[1:]), 0, dim)
            for b, t, dim in zip(pieces, turned, dims)
        )
    )


def from_behind(value, axis, steps):
    count = lax.axis_size(axis)
    leading, last = (max(0, -steps), min(count, count - steps))
    return lax.ppermute(value, axis, [(source, source + steps) for source in range(leading, last)])


def contract_last(left_rows, right_rows):
    return lax.dot_general(
        left_rows, right_rows, (((1,), (1,)), ((), ())), preferred_element_type=jnp.float32
    )


def contract_first(left_rows, right_rows):
    return lax.dot_general(
        left_rows, right_rows, (((0,), (0,)), ((), ())), preferred_element_type=jnp.float32
    )


def prepare(hidden, weight_in):
    widened = hidden.astype(jnp.float32)
    inverse_rms = lax.rsqrt(jnp.mean(widened * widened, axis=-1, keepdims=True) + epsilon)
    normed = (widened * inverse_rms).astype(jnp.bfloat16)
    pre_act = jnp.dot(normed, weight_in, preferred_element_type=jnp.float32)
    activated = jax.nn.silu(pre_act).astype(jnp.bfloat16)
    return (widened, inverse_rms, normed, pre_act, activated)


def advance(hidden, weight_in, weight_out):
    widened, inverse_rms, normed, pre_act, activated = prepare(hidden, weight_in)
    return (widened + jnp.dot(activated, weight_out, preferred_element_type=jnp.float32)).astype(
        jnp.bfloat16
    )


def retreat(hidden, cot_in, weight_in, weight_out):
    widened, inverse_rms, normed, pre_act, activated = prepare(hidden, weight_in)
    act_grad = contract_last(cot_in, weight_out)
    sigmoid_vals = jax.nn.sigmoid(pre_act)
    pre_grad = (act_grad * sigmoid_vals * (1.0 + pre_act * (1.0 - sigmoid_vals))).astype(
        jnp.bfloat16
    )
    norm_grad = contract_last(pre_grad, weight_in)
    unit_rows = widened * inverse_rms
    rms_grad = inverse_rms * (
        norm_grad - unit_rows * jnp.mean(norm_grad * unit_rows, axis=-1, keepdims=True)
    )
    earlier = (cot_in.astype(jnp.float32) + rms_grad).astype(jnp.bfloat16)
    return (earlier, contract_first(normed, pre_grad), contract_first(activated, cot_in))


def shards(hidden_in, out_grad, fast_in, fast_out, slow_in, slow_out):
    sections = lax.axis_size("section")
    section_index = lax.axis_index("section")
    row_count, model_width = hidden_in.shape
    branch_units = fast_in.shape[2]
    in_scale = 1.0 / math.sqrt(model_width)
    out_scale = 1.0 / math.sqrt(branch_units)
    local_in = (fast_in[0] * in_scale).astype(jnp.bfloat16)
    local_out = (fast_out[0] * out_scale).astype(jnp.bfloat16)
    weight_in, weight_out = gather_turned((local_in, local_out), "fsdp", (0, 1))
    portions = 1
    block_rows = row_count // portions
    turn_count = sections + portions - 1
    sources = hidden_in.reshape(portions, block_rows, model_width)
    targets = out_grad.reshape(portions, block_rows, model_width)
    saved_inputs = jnp.zeros_like(sources)
    produced = jnp.zeros_like(sources)
    incoming = jnp.zeros((block_rows, model_width), jnp.bfloat16)
    for timestep in range(turn_count):
        block_slot = timestep - section_index
        active = (block_slot >= 0) & (block_slot < portions)
        block_index = jnp.clip(block_slot, 0, portions - 1)
        first_input = lax.dynamic_index_in_dim(sources, block_index, 0, keepdims=False)
        section_input = jnp.where(section_index == 0, first_input, incoming)

        def run_forward():
            return advance(section_input, weight_in, weight_out)

        def skip_forward():
            return jnp.zeros_like(section_input)

        section_output = lax.cond(active, run_forward, skip_forward)
        saved_inputs = jnp.where(
            active,
            lax.dynamic_update_index_in_dim(saved_inputs, section_input, block_index, 0),
            saved_inputs,
        )
        produced = jnp.where(
            active,
            lax.dynamic_update_index_in_dim(produced, section_output, block_index, 0),
            produced,
        )
        if timestep + 1 < turn_count:
            incoming = from_behind(section_output, "section", 1)
    grad_in = jnp.zeros((model_width, branch_units), jnp.float32)
    grad_out = jnp.zeros((branch_units, model_width), jnp.float32)
    cotangents = jnp.zeros_like(sources)
    incoming = jnp.zeros((block_rows, model_width), jnp.bfloat16)
    for timestep in range(turn_count):
        block_slot = timestep - (sections - 1 - section_index)
        active = (block_slot >= 0) & (block_slot < portions)
        block_index = jnp.clip(block_slot, 0, portions - 1)
        last_cot = lax.dynamic_index_in_dim(targets, block_index, 0, keepdims=False)
        cot_in = jnp.where(section_index == sections - 1, last_cot, incoming)
        hidden = lax.dynamic_index_in_dim(saved_inputs, block_index, 0, keepdims=False)

        def run_backward():
            return retreat(hidden, cot_in, weight_in, weight_out)

        def skip_backward():
            return (
                jnp.zeros_like(cot_in),
                jnp.zeros((model_width, branch_units), jnp.float32),
                jnp.zeros((branch_units, model_width), jnp.float32),
            )

        earlier, term_in, term_out = lax.cond(active, run_backward, skip_backward)
        grad_in = grad_in + term_in
        grad_out = grad_out + term_out
        cotangents = jnp.where(
            active, lax.dynamic_update_index_in_dim(cotangents, earlier, block_index, 0), cotangents
        )
        if timestep + 1 < turn_count:
            incoming = from_behind(earlier, "section", -1)
    shard_in, shard_out = (
        lax.psum_scatter(
            (grad_in * in_scale).astype(jnp.bfloat16), "fsdp", scatter_dimension=0, tiled=True
        ).astype(jnp.float32),
        lax.psum_scatter(
            (grad_out * out_scale).astype(jnp.bfloat16), "fsdp", scatter_dimension=1, tiled=True
        ).astype(jnp.float32),
    )
    fresh_in = fast_in[0] - fast_rate * shard_in
    fresh_out = fast_out[0] - fast_rate * shard_out
    synced_first = slow_in[0] + preview_mix * (fresh_in - slow_in[0])
    synced_second = slow_out[0] + preview_mix * (fresh_out - slow_out[0])
    section_out = produced.reshape(row_count, model_width)[None]
    input_grad = cotangents.reshape(row_count, model_width)[None]
    return (section_out, input_grad, synced_first[None], synced_second[None])


def solution(mesh):
    placed = (
        P("fsdp", None),
        P("fsdp", None),
        P("section", "fsdp", None),
        P("section", None, "fsdp"),
        P("section", "fsdp", None),
        P("section", None, "fsdp"),
    )
    return jax.shard_map(
        shards,
        mesh=mesh,
        in_specs=placed,
        out_specs=(
            P("section", "fsdp", None),
            P("section", "fsdp", None),
            P("section", "fsdp", None),
            P("section", None, "fsdp"),
        ),
        check_vma=False,
    )
```

profile of v0, /device:TPU:0, one launch (start us, length us, event | category | flops | bytes accessed | tf_op | source)
XLA Modules:
  0.0 1018.3 jit_solution(3030344230402729887)
XLA Ops:
  9.7 365.5 %all-gather.2.cloned.1.call-done = bf16[4096,2048]{1,0:T(8,128)(2,1)} async-done(((bf16[128,2048]{1,0:T(8,128)(2,1)}), bf16[4096,2048]{1,0:T(8,128)(2,1)}) %all-gather.2.cloned.1.call-update) | async-done | bytes 16777232 | tf_op jit(solution)/shard_map/all_gather | solution.py:16
  375.2 11.7 %slice_bitcast_fusion = (bf16[1024,4096]{0,1:T(8,128)(2,1)}, bf16[4096,1024]{1,0:T(8,128)(2,1)}) fusion(bf16[4096,2048]{1,0:T(8,128)(2,1)} %all-gather.2.cloned.1.call-done), kind=kLoop, calls=%fused_computation.146 | loop fusion | bytes 33554432 | tf_op jit(solution)/shard_map/transpose | solution.py:20
  386.9 10.2 conditional.8
  387.2 9.9 fusion
  398.5 2.2 collective-permute-done
  401.9 19.2 %collective-permute-start.1 = (bf16[128,4096]{1,0:T(8,128)(2,1)S(1)}, bf16[128,4096]{1,0:T(8,128)(2,1)S(1)}, u32[]{:S(2)}, u32[]{:S(2)}) collective-permute-start(bf16[128,4096]{1,0:T(8,128)(2,1)S(1)} %get-tuple-element.275), channel_id=1, source_target_pairs={{0,32},{32,64},{64,96},{1,33},{33,65},{65,97},{2,34},{34,66},{66,9... | collective-permute-start | bytes 3145736 | tf_op jit(solution)/shard_map/ppermute | solution.py:29
  421.1 2.2 collective-permute-done.1
  424.7 12.4 %collective-permute-start.2 = (bf16[128,4096]{1,0:T(8,128)(2,1)S(1)}, bf16[128,4096]{1,0:T(8,128)(2,1)}, u32[]{:S(2)}, u32[]{:S(2)}) collective-permute-start(bf16[128,4096]{1,0:T(8,128)(2,1)S(1)} %get-tuple-element.276), channel_id=1, source_target_pairs={{0,32},{32,64},{64,96},{1,33},{33,65},{65,97},{2,34},{34,66},{66,9... | collective-permute-start | bytes 3145736 | tf_op jit(solution)/shard_map/ppermute | solution.py:29
  439.7 16.1 %conditional.12 = (bf16[128,4096]{1,0:T(8,128)(2,1)S(1)}, f32[4096,1024]{1,0:T(8,128)}, f32[1024,4096]{0,1:T(8,128)}) conditional(s32[]{:T(128)} %convert_element_type.171, () %tuple.75, (pred[]{:T(512)}, bf16[128,4096]{1,0:T(8,128)(2,1)S(1)}, bf16[128,4096]{1,0:T(8,128)(2,1)S(1)}, bf16[128,4096]{1,0:T(8,128)(2,1)S(1)}, ...), branch_computations={%region_12.13_spmd, %region_13.16_spmd} | conditional | flops 5382078464 | bytes 128194168 | solution.py:142
  439.8 7.9 broadcast.228
  447.7 7.9 broadcast.229.clone
  457.2 29.5 %collective-permute-done.3 = bf16[128,4096]{1,0:T(8,128)(2,1)} collective-permute-done((bf16[128,4096]{1,0:T(8,128)(2,1)S(1)}, bf16[128,4096]{1,0:T(8,128)(2,1)}, u32[]{:S(2)}, u32[]{:S(2)}) %collective-permute-start.3) | collective-permute-done | bytes 1048608 | tf_op jit(solution)/shard_map/ppermute | solution.py:29
  486.7 16.4 %conditional.13 = (bf16[128,4096]{1,0:T(8,128)(2,1)S(1)}, f32[4096,1024]{1,0:T(8,128)}, f32[1024,4096]{0,1:T(8,128)}) conditional(s32[]{:T(128)} %convert_element_type.170, () %tuple.74, (pred[]{:T(512)}, bf16[128,4096]{1,0:T(8,128)(2,1)S(1)}, bf16[128,4096]{1,0:T(8,128)(2,1)}, bf16[128,4096]{1,0:T(8,128)(2,1)S(1)}, bf16[1024,4096]{0,1:T(8,128)(2,1)}, ...), branch_computations={%region_16.17_spmd, %region_17.20_spmd} | conditional | flops 5382078464 | bytes 128194168 | solution.py:142
  487.1 8.0 broadcast.234
  495.1 8.0 broadcast.235.clone
  504.5 17.3 %collective-permute-done.4 = bf16[128,4096]{1,0:T(8,128)(2,1)} collective-permute-done((bf16[128,4096]{1,0:T(8,128)(2,1)S(1)}, bf16[128,4096]{1,0:T(8,128)(2,1)}, u32[]{:S(2)}, u32[]{:S(2)}) %collective-permute-start.4) | collective-permute-done | bytes 1048608 | tf_op jit(solution)/shard_map/ppermute | solution.py:29
  521.7 17.0 %conditional.14 = (bf16[128,4096]{1,0:T(8,128)(2,1)}, f32[4096,1024]{1,0:T(8,128)}, f32[1024,4096]{0,1:T(8,128)}) conditional(s32[]{:T(128)} %convert_element_type.169, () %tuple.73, (pred[]{:T(512)}, bf16[128,4096]{1,0:T(8,128)(2,1)S(1)}, bf16[128,4096]{1,0:T(8,128)(2,1)}, bf16[128,4096]{1,0:T(8,128)(2,1)S(1)}, bf16[1024,4096]{0,1:T(8,128)(2,1)}, ...), branch_computations={%region_20.21_spmd, %region_21.24_spmd} | conditional | flops 5382078464 | bytes 128194168 | solution.py:142
  521.9 7.9 broadcast.240
  529.8 7.9 broadcast.241.clone
  540.0 37.3 %collective-permute-done.5 = bf16[128,4096]{1,0:T(8,128)(2,1)} collective-permute-done((bf16[128,4096]{1,0:T(8,128)(2,1)}, bf16[128,4096]{1,0:T(8,128)(2,1)}, u32[]{:S(2)}, u32[]{:S(2)}) %collective-permute-start.5) | collective-permute-done | bytes 1048608 | tf_op jit(solution)/shard_map/ppermute | solution.py:29
  577.4 29.4 %conditional.15 = (bf16[128,4096]{1,0:T(8,128)(2,1)}, f32[4096,1024]{1,0:T(8,128)}, f32[1024,4096]{0,1:T(8,128)}) conditional(s32[]{:T(128)} %convert_element_type.168, () %tuple.72, (pred[]{:T(512)}, bf16[128,4096]{1,0:T(8,128)(2,1)S(1)}, bf16[128,4096]{1,0:T(8,128)(2,1)}, bf16[128,4096]{1,0:T(8,128)(2,1)S(1)}, bf16[1024,4096]{0,1:T(8,128)(2,1)}, ...), branch_computations={%region_24.25_spmd, %region_25.28_spmd} | conditional | flops 5382078464 | bytes 128194168 | solution.py:142
  577.9 4.8 fusion.115
  585.6 8.2 fusion.113
  593.8 3.0 fusion.105
  596.8 1.6 fusion.109
  598.4 8.1 fusion.117
  606.8 26.0 %multiply_convert_fusion.12 = bf16[1024,4096]{0,1:T(8,128)(2,1)} fusion(f32[1024,4096]{0,1:T(8,128)} %get-tuple-element.235, f32[1024,4096]{0,1:T(8,128)} %get-tuple-element.234, f32[1024,4096]{0,1:T(8,128)} %get-tuple-element.232, f32[1024,4096]{0,1:T(8,128)} %get-tuple-element.233), kind=kLoop, calls=%fused_computation.144 | loop fusion | flops 20971520 | bytes 75497472 | tf_op jit(solution)/shard_map/convert_element_type | solution.py:155
  632.8 26.3 %multiply_convert_fusion.13 = bf16[4096,1024]{1,0:T(8,128)(2,1)} fusion(f32[4096,1024]{1,0:T(8,128)} %get-tuple-element.151, f32[4096,1024]{1,0:T(8,128)} %get-tuple-element.150, f32[4096,1024]{1,0:T(8,128)} %get-tuple-element.148, f32[4096,1024]{1,0:T(8,128)} %get-tuple-element.149), kind=kLoop, calls=%fused_computation.145 | loop fusion | flops 20971520 | bytes 75497472 | tf_op jit(solution)/shard_map/convert_element_type | solution.py:152
  662.8 3.3 select_bitcast_fusion
  666.1 152.7 %reduce-scatter.5.cloned.1.call-done = bf16[1024,128]{0,1:T(8,128)(2,1)} async-done(((bf16[1024,4096]{0,1:T(8,128)(2,1)}), bf16[1024,128]{0,1:T(8,128)(2,1)}) %reduce-scatter.5.cloned.1.call-update) | async-done | bytes 262160 | tf_op jit(solution)/shard_map/reduce_scatter | solution.py:154
  820.9 188.6 %reduce-scatter.3.cloned.1.call-done = bf16[128,1024]{1,0:T(8,128)(2,1)} async-done(((bf16[4096,1024]{1,0:T(8,128)(2,1)}), bf16[128,1024]{1,0:T(8,128)(2,1)}) %reduce-scatter.3.cloned.1.call-update) | async-done | bytes 262160 | tf_op jit(solution)/shard_map/reduce_scatter | solution.py:151
  1009.5 1.9 fusion.123
  (79 shorter events, 23.7 us)
Async XLA Ops:
  7.2 1.5 copy-start.10
  7.2 2.5 copy-start.1
  7.2 368.1 %all-gather.2.cloned.1.call-start = ((), (), s32[]{:S(2)}) async-start(), calls=%async_computation.2 | async-start | bytes 17301504 | tf_op jit(solution)/shard_map/all_gather | solution.py:16
  8.6 1.1 copy-start.2
  9.6 809.3 %reduce-scatter.5.cloned.1.call-start = ((), (), s32[]{:S(2)}) async-start(), calls=%async_computation.4 | async-start | bytes 8650752 | tf_op jit(solution)/shard_map/reduce_scatter | solution.py:154
  397.1 4.7 copy-start.6
  397.1 3.6 collective-permute-start
  401.9 22.5 %copy-start.7 = (bf16[128,4096]{1,0:T(8,128)(2,1)}, bf16[128,4096]{1,0:T(8,128)(2,1)S(1)}, u32[]{:S(2)}) copy-start(bf16[128,4096]{1,0:T(8,128)(2,1)S(1)} %get-tuple-element.275) | copy-start | bytes 3145732
  401.9 21.4 %collective-permute-start.1 = (bf16[128,4096]{1,0:T(8,128)(2,1)S(1)}, bf16[128,4096]{1,0:T(8,128)(2,1)S(1)}, u32[]{:S(2)}, u32[]{:S(2)}) collective-permute-start(bf16[128,4096]{1,0:T(8,128)(2,1)S(1)} %get-tuple-element.275), channel_id=1, source_target_pairs={{0,32},{32,64},{64,96},{1,33},{33,65},{65,97},{2,34},{34,66},{66,9... | collective-permute-start | bytes 3145736 | tf_op jit(solution)/shard_map/ppermute | solution.py:29
  424.7 12.4 %copy-start.8 = (bf16[128,4096]{1,0:T(8,128)(2,1)}, bf16[128,4096]{1,0:T(8,128)(2,1)S(1)}, u32[]{:S(2)}) copy-start(bf16[128,4096]{1,0:T(8,128)(2,1)S(1)} %get-tuple-element.276) | copy-start | bytes 3145732
  424.7 13.8 %collective-permute-start.2 = (bf16[128,4096]{1,0:T(8,128)(2,1)S(1)}, bf16[128,4096]{1,0:T(8,128)(2,1)}, u32[]{:S(2)}, u32[]{:S(2)}) collective-permute-start(bf16[128,4096]{1,0:T(8,128)(2,1)S(1)} %get-tuple-element.276), channel_id=1, source_target_pairs={{0,32},{32,64},{64,96},{1,33},{33,65},{65,97},{2,34},{34,66},{66,9... | collective-permute-start | bytes 3145736 | tf_op jit(solution)/shard_map/ppermute | solution.py:29
  437.0 2.7 copy-start
  455.9 30.8 %copy-start.4 = (bf16[128,4096]{1,0:T(8,128)(2,1)}, bf16[128,4096]{1,0:T(8,128)(2,1)S(1)}, u32[]{:S(2)}) copy-start(bf16[128,4096]{1,0:T(8,128)(2,1)S(1)} %get-tuple-element.144) | copy-start | bytes 3145732
  455.9 30.8 %collective-permute-start.3 = (bf16[128,4096]{1,0:T(8,128)(2,1)S(1)}, bf16[128,4096]{1,0:T(8,128)(2,1)}, u32[]{:S(2)}, u32[]{:S(2)}) collective-permute-start(bf16[128,4096]{1,0:T(8,128)(2,1)S(1)} %get-tuple-element.144), channel_id=1, source_target_pairs={{32,0},{64,32},{96,64},{33,1},{65,33},{97,65},{34,2},{66,34},{98,6... | collective-permute-start | bytes 3145736 | tf_op jit(solution)/shard_map/ppermute | solution.py:29
  503.2 18.6 %collective-permute-start.4 = (bf16[128,4096]{1,0:T(8,128)(2,1)S(1)}, bf16[128,4096]{1,0:T(8,128)(2,1)}, u32[]{:S(2)}, u32[]{:S(2)}) collective-permute-start(bf16[128,4096]{1,0:T(8,128)(2,1)S(1)} %get-tuple-element.145), channel_id=1, source_target_pairs={{32,0},{64,32},{96,64},{33,1},{65,33},{97,65},{34,2},{66,34},{98,6... | collective-permute-start | bytes 3145736 | tf_op jit(solution)/shard_map/ppermute | solution.py:29
  538.7 38.6 %collective-permute-start.5 = (bf16[128,4096]{1,0:T(8,128)(2,1)}, bf16[128,4096]{1,0:T(8,128)(2,1)}, u32[]{:S(2)}, u32[]{:S(2)}) collective-permute-start(bf16[128,4096]{1,0:T(8,128)(2,1)} %get-tuple-element.146), channel_id=1, source_target_pairs={{32,0},{64,32},{96,64},{33,1},{65,33},{97,65},{34,2},{66,34},{98,6... | collective-permute-start | bytes 3145736 | tf_op jit(solution)/shard_map/ppermute | solution.py:29
  577.9 6.2 slice-start.14
  577.9 6.2 slice-start.15
  584.1 9.7 slice-start.6
  585.6 8.2 slice-start.7
  632.8 376.7 %reduce-scatter.3.cloned.1.call-start = ((), (), s32[]{:S(2)}) async-start(), calls=%async_computation.3 | async-start | bytes 8650752 | tf_op jit(solution)/shard_map/reduce_scatter | solution.py:151
  659.1 1.0 copy-start.14
  661.2 1.6 copy-start.5
  661.3 1.0 copy-start.9
  662.8 156.1 %copy-start.3 = (f32[1,1024,128]{1,2,0:T(8,128)S(1)}, f32[1,1024,128]{1,2,0:T(8,128)}, u32[]{:S(2)}) copy-start(f32[1,1024,128]{1,2,0:T(8,128)} %copy-done.2) | copy-start | bytes 1572868
  662.8 156.1 %copy-start.12 = (f32[1,1024,128]{1,2,0:T(8,128)S(1)}, f32[1,1024,128]{1,2,0:T(8,128)}, u32[]{:S(2)}) copy-start(f32[1,1024,128]{1,2,0:T(8,128)} %copy.33) | copy-start | bytes 1572868
  666.1 343.4 %copy-start.11 = (f32[1,128,1024]{2,1,0:T(8,128)S(1)}, f32[1,128,1024]{2,1,0:T(8,128)}, u32[]{:S(2)}) copy-start(f32[1,128,1024]{2,1,0:T(8,128)} %param.24) | copy-start | bytes 1572868
  666.1 343.4 %copy-start.13 = (f32[1,128,1024]{2,1,0:T(8,128)S(1)}, f32[1,128,1024]{2,1,0:T(8,128)}, u32[]{:S(2)}) copy-start(f32[1,128,1024]{2,1,0:T(8,128)} %param.26) | copy-start | bytes 1572868
Sparse Core Ops, SparseCore 0:
  10.2 364.9 all-gather.1
  632.9 185.8 reduce-scatter.4
  821.3 188.1 reduce-scatter.2
where the time goes:
time: 1030 us; the launch traced here: 1020 us
  waiting for transfers between devices  797 us (77%)
  local copies, waits for them, and re-layouts  66.7 us (6%)
  other arithmetic  66.4 us (6%)
  starting transfers between devices  36.9 us (4%)
  matrix products  35.5 us (3%)
  between operations  14.5 us (1%)
    all_gather x1, waiting for transfers between devices, gather_turned(): result = lax.all_gather(both, axis, axis=0, tiled=True)  366 us
    reduce_scatter x1, waiting for transfers between devices, shards(): lax.psum_scatter((grad_in * in_scale).astype(jnp.bfloat16), 'fsdp', scatt...  189 us
    reduce_scatter x1, waiting for transfers between devices, shards(): lax.psum_scatter((grad_out * out_scale).astype(jnp.bfloat16), 'fsdp', sca...  153 us
    ppermute x6, waiting for transfers between devices, from_behind(): lax.ppermute(value, axis, [(source, source + steps) for source in range(l...  89.9 us
    another operation x13, local copies, waits for them, and re-layouts  49.1 us
    ppermute x6, starting transfers between devices, from_behind(): lax.ppermute(value, axis, [(source, source + steps) for source in range(l...  36.8 us
    convert_element_type x1, other arithmetic, shards(): (grad_in * in_scale).astype(jnp.bfloat16)  26.3 us
    convert_element_type x1, other arithmetic, shards(): (grad_out * out_scale).astype(jnp.bfloat16)  26 us
  transfers between devices with their start and end apart: 9, of which 9 were waited for; matrix products, arithmetic and copies ran while one was open for 3% of the time, Pallas kernels for 0%

commit v1 on v0

--- a/solution.py
+++ b/solution.py
@@ -3,6 +3,7 @@
 import jax.numpy as jnp
 from jax import lax
 from jax.sharding import PartitionSpec as P
+from jax.lax import all_to_all, axis_size
 
 epsilon = 1e-05
 fast_rate = 0.5
@@ -13,7 +14,9 @@
     turned = [jnp.moveaxis(a, dim, 0) for a, dim in zip(arrays, dims)]
     widths = [t[0].size for t in turned]
     both = jnp.concatenate([t.reshape(-1, w) for t, w in zip(turned, widths)], axis=1)
-    result = lax.all_gather(both, axis, axis=0, tiled=True)
+    result = jnp.concatenate(
+        all_to_all(jnp.stack([both for _ in range(axis_size(axis))], 0), axis, 0, 0), 0
+    )
     pieces = jnp.split(result, [sum(widths[:k]) for k in range(1, len(widths))], axis=1)
     return tuple(
         (

time: 1030 us -> 956 us (0.928)
  waiting for transfers between devices: 797 us -> 715 us
    all_gather x1 -> x0, waiting for transfers between devices: 366 us -> none  [gather_turned(): result = lax.all_gather(both, axis, axis=0, tiled=True)]
    all_to_all x0 -> x1, waiting for transfers between devices: none -> 269 us  [gather_turned(): all_to_all(jnp.stack([both for _ in range(axis_size(axis))], 0), axis, 0, 0)]
    reduce_scatter x1, waiting for transfers between devices: 153 us -> 167 us  [shards(): lax.psum_scatter((grad_out * out_scale).astype(jnp.bfloat16), 'fsdp', sca...]
    another operation x13 -> x14, local copies, waits for them, and re-layouts: 49.1 us -> 55.3 us
where the time goes in v1:
time: 956 us; the launch traced here: 949 us
  waiting for transfers between devices  715 us (75%)
  local copies, waits for them, and re-layouts  72.8 us (8%)
  other arithmetic  65.3 us (7%)
  starting transfers between devices  44 us (5%)
  matrix products  35.5 us (4%)
  between operations  14.8 us (2%)
    all_to_all x1, waiting for transfers between devices, gather_turned(): all_to_all(jnp.stack([both for _ in range(axis_size(axis))], 0), axis, 0, 0)  269 us
    reduce_scatter x1, waiting for transfers between devices, shards(): lax.psum_scatter((grad_in * in_scale).astype(jnp.bfloat16), 'fsdp', scatt...  188 us
    reduce_scatter x1, waiting for transfers between devices, shards(): lax.psum_scatter((grad_out * out_scale).astype(jnp.bfloat16), 'fsdp', sca...  167 us
    ppermute x6, waiting for transfers between devices, from_behind(): lax.ppermute(value, axis, [(source, source + steps) for source in range(l...  89.9 us
    another operation x13, local copies, waits for them, and re-layouts  49.2 us
    ppermute x6, starting transfers between devices, from_behind(): lax.ppermute(value, axis, [(source, source + steps) for source in range(l...  34.4 us
    convert_element_type x1, other arithmetic, shards(): (grad_in * in_scale).astype(jnp.bfloat16)  26.1 us
    convert_element_type x1, other arithmetic, shards(): (grad_out * out_scale).astype(jnp.bfloat16)  26 us
  transfers between devices with their start and end apart: 9, of which 9 were waited for; matrix products, arithmetic and copies ran while one was open for 3% of the time, Pallas kernels for 0%

profile of v1, /device:TPU:0, one launch (start us, length us, event | category | flops | bytes accessed | tf_op | source)
XLA Modules:
  0.0 948.7 jit_solution(2325944529418079807)
XLA Ops:
  8.6 6.1 stack.2
  14.8 9.5 %all-to-all-start = ((bf16[32,128,2048]{2,1,0:T(8,128)(2,1)}), bf16[32,128,2048]{2,1,0:T(8,128)(2,1)}, u32[]{:S(2)}, u32[]{:S(2)}) async-start(bf16[32,128,2048]{2,1,0:T(8,128)(2,1)} %stack.2), calls=%async_computation | async-start | bytes 33554432 | tf_op jit(solution)/shard_map/all_to_all | solution.py:18
  24.5 269.1 %all-to-all-done = bf16[32,128,2048]{2,1,0:T(8,128)(2,1)} async-done(((bf16[32,128,2048]{2,1,0:T(8,128)(2,1)}), bf16[32,128,2048]{2,1,0:T(8,128)(2,1)}, u32[]{:S(2)}, u32[]{:S(2)}) %all-to-all-start) | async-done | bytes 16777248 | tf_op jit(solution)/shard_map/all_to_all | solution.py:18
  293.6 11.7 %slice_bitcast_fusion = (bf16[1024,4096]{0,1:T(8,128)(2,1)}, bf16[4096,1024]{1,0:T(8,128)(2,1)}) fusion(bf16[4096,2048]{1,0:T(8,128)(2,1)} %bitcast.3), kind=kLoop, calls=%fused_computation.146 | loop fusion | bytes 33554432 | tf_op jit(solution)/shard_map/transpose | solution.py:23
  305.3 10.2 %conditional.8 = (bf16[128,4096]{1,0:T(8,128)(2,1)S(1)}) conditional(s32[]{:T(128)} %convert_element_type.165, () %tuple.67, (bf16[128,4096]{1,0:T(8,128)(2,1)S(1)}, bf16[4096,1024]{1,0:T(8,128)(2,1)}, bf16[1024,4096]{0,1:T(8,128)(2,1)}) %tuple.68), branch_computations={%region_0.1_spmd, %region_1.3_spmd} | conditional | flops 2152857600 | bytes 19925000 | solution.py:110
  305.6 9.9 %fusion = bf16[128,4096]{1,0:T(8,128)(2,1)S(1)} fusion(bf16[1024,4096]{0,1:T(8,128)(2,1)} %get-tuple-element.194, bf16[128,4096]{1,0:T(8,128)(2,1)S(1)} %get-tuple-element.92, bf16[4096,1024]{1,0:T(8,128)(2,1)} %get-tuple-element.93, f32[128]{0:T(128)S(1)} %add_rsqrt_fusion), kind=kOutput, calls=%fused_computation.1 | convolution fusion | flops 2151284736 | bytes 18874880 | tf_op jit(solution)/shard_map/cond/branch_1_fun/dot_general | solution.py:58
  316.8 2.2 collective-permute-done
  320.2 16.8 %collective-permute-start.1 = (bf16[128,4096]{1,0:T(8,128)(2,1)S(1)}, bf16[128,4096]{1,0:T(8,128)(2,1)S(1)}, u32[]{:S(2)}, u32[]{:S(2)}) collective-permute-start(bf16[128,4096]{1,0:T(8,128)(2,1)S(1)} %get-tuple-element.275), channel_id=1, source_target_pairs={{0,32},{32,64},{64,96},{1,33},{33,65},{65,97},{2,34},{34,66},{66,9... | collective-permute-start | bytes 3145736 | tf_op jit(solution)/shard_map/ppermute | solution.py:32
  337.0 2.2 collective-permute-done.1
  340.6 12.4 %collective-permute-start.2 = (bf16[128,4096]{1,0:T(8,128)(2,1)S(1)}, bf16[128,4096]{1,0:T(8,128)(2,1)}, u32[]{:S(2)}, u32[]{:S(2)}) collective-permute-start(bf16[128,4096]{1,0:T(8,128)(2,1)S(1)} %get-tuple-element.276), channel_id=1, source_target_pairs={{0,32},{32,64},{64,96},{1,33},{33,65},{65,97},{2,34},{34,66},{66,9... | collective-permute-start | bytes 3145736 | tf_op jit(solution)/shard_map/ppermute | solution.py:32
  355.7 16.1 %conditional.12 = (bf16[128,4096]{1,0:T(8,128)(2,1)S(1)}, f32[4096,1024]{1,0:T(8,128)}, f32[1024,4096]{0,1:T(8,128)}) conditional(s32[]{:T(128)} %convert_element_type.171, () %tuple.75, (pred[]{:T(512)}, bf16[128,4096]{1,0:T(8,128)(2,1)S(1)}, bf16[128,4096]{1,0:T(8,128)(2,1)S(1)}, bf16[128,4096]{1,0:T(8,128)(2,1)S(1)}, ...), branch_computations={%region_12.13_spmd, %region_13.16_spmd} | conditional | flops 5382078464 | bytes 128194168 | solution.py:145
  355.7 7.9 broadcast.230
  363.6 7.9 broadcast.231.clone
  373.1 29.5 %collective-permute-done.3 = bf16[128,4096]{1,0:T(8,128)(2,1)} collective-permute-done((bf16[128,4096]{1,0:T(8,128)(2,1)S(1)}, bf16[128,4096]{1,0:T(8,128)(2,1)}, u32[]{:S(2)}, u32[]{:S(2)}) %collective-permute-start.3) | collective-permute-done | bytes 1048608 | tf_op jit(solution)/shard_map/ppermute | solution.py:32
  402.6 16.5 %conditional.13 = (bf16[128,4096]{1,0:T(8,128)(2,1)S(1)}, f32[4096,1024]{1,0:T(8,128)}, f32[1024,4096]{0,1:T(8,128)}) conditional(s32[]{:T(128)} %convert_element_type.170, () %tuple.74, (pred[]{:T(512)}, bf16[128,4096]{1,0:T(8,128)(2,1)S(1)}, bf16[128,4096]{1,0:T(8,128)(2,1)}, bf16[128,4096]{1,0:T(8,128)(2,1)S(1)}, bf16[1024,4096]{0,1:T(8,128)(2,1)}, ...), branch_computations={%region_16.17_spmd, %region_17.20_spmd} | conditional | flops 5382078464 | bytes 128194168 | solution.py:145
  403.0 8.0 broadcast.236
  411.0 8.0 broadcast.237.clone
  420.4 17.3 %collective-permute-done.4 = bf16[128,4096]{1,0:T(8,128)(2,1)} collective-permute-done((bf16[128,4096]{1,0:T(8,128)(2,1)S(1)}, bf16[128,4096]{1,0:T(8,128)(2,1)}, u32[]{:S(2)}, u32[]{:S(2)}) %collective-permute-start.4) | collective-permute-done | bytes 1048608 | tf_op jit(solution)/shard_map/ppermute | solution.py:32
  437.7 17.0 %conditional.14 = (bf16[128,4096]{1,0:T(8,128)(2,1)}, f32[4096,1024]{1,0:T(8,128)}, f32[1024,4096]{0,1:T(8,128)}) conditional(s32[]{:T(128)} %convert_element_type.169, () %tuple.73, (pred[]{:T(512)}, bf16[128,4096]{1,0:T(8,128)(2,1)S(1)}, bf16[128,4096]{1,0:T(8,128)(2,1)}, bf16[128,4096]{1,0:T(8,128)(2,1)S(1)}, bf16[1024,4096]{0,1:T(8,128)(2,1)}, ...), branch_computations={%region_20.21_spmd, %region_21.24_spmd} | conditional | flops 5382078464 | bytes 128194168 | solution.py:145
  437.9 7.9 broadcast.242
  445.7 7.9 broadcast.243.clone
  456.0 37.3 %collective-permute-done.5 = bf16[128,4096]{1,0:T(8,128)(2,1)} collective-permute-done((bf16[128,4096]{1,0:T(8,128)(2,1)}, bf16[128,4096]{1,0:T(8,128)(2,1)}, u32[]{:S(2)}, u32[]{:S(2)}) %collective-permute-start.5) | collective-permute-done | bytes 1048608 | tf_op jit(solution)/shard_map/ppermute | solution.py:32
  493.3 29.4 %conditional.15 = (bf16[128,4096]{1,0:T(8,128)(2,1)}, f32[4096,1024]{1,0:T(8,128)}, f32[1024,4096]{0,1:T(8,128)}) conditional(s32[]{:T(128)} %convert_element_type.168, () %tuple.72, (pred[]{:T(512)}, bf16[128,4096]{1,0:T(8,128)(2,1)S(1)}, bf16[128,4096]{1,0:T(8,128)(2,1)}, bf16[128,4096]{1,0:T(8,128)(2,1)S(1)}, bf16[1024,4096]{0,1:T(8,128)(2,1)}, ...), branch_computations={%region_24.25_spmd, %region_25.28_spmd} | conditional | flops 5382078464 | bytes 128194168 | solution.py:145
  493.8 4.8 fusion.115
  501.6 8.2 fusion.113
  509.8 3.0 fusion.105
  514.3 8.1 fusion.117
  522.7 26.0 %multiply_convert_fusion.12 = bf16[1024,4096]{0,1:T(8,128)(2,1)} fusion(f32[1024,4096]{0,1:T(8,128)} %get-tuple-element.235, f32[1024,4096]{0,1:T(8,128)} %get-tuple-element.234, f32[1024,4096]{0,1:T(8,128)} %get-tuple-element.232, f32[1024,4096]{0,1:T(8,128)} %get-tuple-element.233), kind=kLoop, calls=%fused_computation.144 | loop fusion | flops 20971520 | bytes 75497472 | tf_op jit(solution)/shard_map/convert_element_type | solution.py:158
  548.8 26.1 %multiply_convert_fusion.13 = bf16[4096,1024]{1,0:T(8,128)(2,1)} fusion(f32[4096,1024]{1,0:T(8,128)} %get-tuple-element.151, f32[4096,1024]{1,0:T(8,128)} %get-tuple-element.150, f32[4096,1024]{1,0:T(8,128)} %get-tuple-element.148, f32[4096,1024]{1,0:T(8,128)} %get-tuple-element.149), kind=kLoop, calls=%fused_computation.145 | loop fusion | flops 20971520 | bytes 75497472 | tf_op jit(solution)/shard_map/convert_element_type | solution.py:155
  578.5 3.3 select_bitcast_fusion
  581.8 167.4 %reduce-scatter.5.cloned.1.call-done = bf16[1024,128]{0,1:T(8,128)(2,1)} async-done(((bf16[1024,4096]{0,1:T(8,128)(2,1)}), bf16[1024,128]{0,1:T(8,128)(2,1)}) %reduce-scatter.5.cloned.1.call-update) | async-done | bytes 262160 | tf_op jit(solution)/shard_map/reduce_scatter | solution.py:157
  751.3 188.3 %reduce-scatter.3.cloned.1.call-done = bf16[128,1024]{1,0:T(8,128)(2,1)} async-done(((bf16[4096,1024]{1,0:T(8,128)(2,1)}), bf16[128,1024]{1,0:T(8,128)(2,1)}) %reduce-scatter.3.cloned.1.call-update) | async-done | bytes 262160 | tf_op jit(solution)/shard_map/reduce_scatter | solution.py:154
  (79 shorter events, 26.2 us)
Async XLA Ops:
  7.2 1.4 copy-start.10
  8.5 6.3 copy-start.2
  14.8 9.6 %copy-start.1 = (bf16[128,4096]{1,0:T(8,128)(2,1)S(1)}, bf16[128,4096]{1,0:T(8,128)(2,1)}, u32[]{:S(2)}) copy-start(bf16[128,4096]{1,0:T(8,128)(2,1)} %param.22) | copy-start | bytes 3145732
  14.8 278.8 %all-to-all-start = ((bf16[32,128,2048]{2,1,0:T(8,128)(2,1)}), bf16[32,128,2048]{2,1,0:T(8,128)(2,1)}, u32[]{:S(2)}, u32[]{:S(2)}) async-start(bf16[32,128,2048]{2,1,0:T(8,128)(2,1)} %stack.2), calls=%async_computation | async-start | bytes 33554432 | tf_op jit(solution)/shard_map/all_to_all | solution.py:18
  24.3 724.9 %reduce-scatter.5.cloned.1.call-start = ((), (), s32[]{:S(2)}) async-start(), calls=%async_computation.4 | async-start | bytes 8650752 | tf_op jit(solution)/shard_map/reduce_scatter | solution.py:157
  315.5 4.7 copy-start.6
  315.5 3.6 collective-permute-start
  320.2 20.1 %copy-start.7 = (bf16[128,4096]{1,0:T(8,128)(2,1)}, bf16[128,4096]{1,0:T(8,128)(2,1)S(1)}, u32[]{:S(2)}) copy-start(bf16[128,4096]{1,0:T(8,128)(2,1)S(1)} %get-tuple-element.275) | copy-start | bytes 3145732
  320.2 19.0 %collective-permute-start.1 = (bf16[128,4096]{1,0:T(8,128)(2,1)S(1)}, bf16[128,4096]{1,0:T(8,128)(2,1)S(1)}, u32[]{:S(2)}, u32[]{:S(2)}) collective-permute-start(bf16[128,4096]{1,0:T(8,128)(2,1)S(1)} %get-tuple-element.275), channel_id=1, source_target_pairs={{0,32},{32,64},{64,96},{1,33},{33,65},{65,97},{2,34},{34,66},{66,9... | collective-permute-start | bytes 3145736 | tf_op jit(solution)/shard_map/ppermute | solution.py:32
  340.6 12.4 %copy-start.8 = (bf16[128,4096]{1,0:T(8,128)(2,1)}, bf16[128,4096]{1,0:T(8,128)(2,1)S(1)}, u32[]{:S(2)}) copy-start(bf16[128,4096]{1,0:T(8,128)(2,1)S(1)} %get-tuple-element.276) | copy-start | bytes 3145732
  340.6 13.8 %collective-permute-start.2 = (bf16[128,4096]{1,0:T(8,128)(2,1)S(1)}, bf16[128,4096]{1,0:T(8,128)(2,1)}, u32[]{:S(2)}, u32[]{:S(2)}) collective-permute-start(bf16[128,4096]{1,0:T(8,128)(2,1)S(1)} %get-tuple-element.276), channel_id=1, source_target_pairs={{0,32},{32,64},{64,96},{1,33},{33,65},{65,97},{2,34},{34,66},{66,9... | collective-permute-start | bytes 3145736 | tf_op jit(solution)/shard_map/ppermute | solution.py:32
  353.0 2.7 copy-start
  371.8 30.8 %copy-start.4 = (bf16[128,4096]{1,0:T(8,128)(2,1)}, bf16[128,4096]{1,0:T(8,128)(2,1)S(1)}, u32[]{:S(2)}) copy-start(bf16[128,4096]{1,0:T(8,128)(2,1)S(1)} %get-tuple-element.144) | copy-start | bytes 3145732
  371.8 30.8 %collective-permute-start.3 = (bf16[128,4096]{1,0:T(8,128)(2,1)S(1)}, bf16[128,4096]{1,0:T(8,128)(2,1)}, u32[]{:S(2)}, u32[]{:S(2)}) collective-permute-start(bf16[128,4096]{1,0:T(8,128)(2,1)S(1)} %get-tuple-element.144), channel_id=1, source_target_pairs={{32,0},{64,32},{96,64},{33,1},{65,33},{97,65},{34,2},{66,34},{98,6... | collective-permute-start | bytes 3145736 | tf_op jit(solution)/shard_map/ppermute | solution.py:32
  419.1 18.6 %collective-permute-start.4 = (bf16[128,4096]{1,0:T(8,128)(2,1)S(1)}, bf16[128,4096]{1,0:T(8,128)(2,1)}, u32[]{:S(2)}, u32[]{:S(2)}) collective-permute-start(bf16[128,4096]{1,0:T(8,128)(2,1)S(1)} %get-tuple-element.145), channel_id=1, source_target_pairs={{32,0},{64,32},{96,64},{33,1},{65,33},{97,65},{34,2},{66,34},{98,6... | collective-permute-start | bytes 3145736 | tf_op jit(solution)/shard_map/ppermute | solution.py:32
  454.7 38.6 %collective-permute-start.5 = (bf16[128,4096]{1,0:T(8,128)(2,1)}, bf16[128,4096]{1,0:T(8,128)(2,1)}, u32[]{:S(2)}, u32[]{:S(2)}) collective-permute-start(bf16[128,4096]{1,0:T(8,128)(2,1)} %get-tuple-element.146), channel_id=1, source_target_pairs={{32,0},{64,32},{96,64},{33,1},{65,33},{97,65},{34,2},{66,34},{98,6... | collective-permute-start | bytes 3145736 | tf_op jit(solution)/shard_map/ppermute | solution.py:32
  493.8 6.2 slice-start.14
  493.8 6.2 slice-start.15
  500.0 9.7 %slice-start.6 = ((s8[8388608]{0:T(1024)(128)(4,1)}), s8[4194304]{0:T(1024)(128)(4,1)S(1)}, s32[]{:S(2)}) async-start(s8[8388608]{0:T(1024)(128)(4,1)} %bitcast.89), calls=%async_computation.11 | async-start | bytes 8388608 | tf_op jit(solution)/shard_map/cond
  501.5 8.2 slice-start.7
  548.7 390.9 %reduce-scatter.3.cloned.1.call-start = ((), (), s32[]{:S(2)}) async-start(), calls=%async_computation.3 | async-start | bytes 8650752 | tf_op jit(solution)/shard_map/reduce_scatter | solution.py:154
  574.9 1.0 copy-start.14
  576.9 1.6 copy-start.5
  577.0 1.0 copy-start.9
  578.5 170.7 %copy-start.3 = (f32[1,1024,128]{1,2,0:T(8,128)S(1)}, f32[1,1024,128]{1,2,0:T(8,128)}, u32[]{:S(2)}) copy-start(f32[1,1024,128]{1,2,0:T(8,128)} %copy-done.2) | copy-start | bytes 1572868
  578.5 170.7 %copy-start.12 = (f32[1,1024,128]{1,2,0:T(8,128)S(1)}, f32[1,1024,128]{1,2,0:T(8,128)}, u32[]{:S(2)}) copy-start(f32[1,1024,128]{1,2,0:T(8,128)} %copy.34) | copy-start | bytes 1572868
  581.8 357.8 %copy-start.11 = (f32[1,128,1024]{2,1,0:T(8,128)S(1)}, f32[1,128,1024]{2,1,0:T(8,128)}, u32[]{:S(2)}) copy-start(f32[1,128,1024]{2,1,0:T(8,128)} %param.24) | copy-start | bytes 1572868
  581.8 357.8 %copy-start.13 = (f32[1,128,1024]{2,1,0:T(8,128)S(1)}, f32[1,128,1024]{2,1,0:T(8,128)}, u32[]{:S(2)}) copy-start(f32[1,128,1024]{2,1,0:T(8,128)} %param.26) | copy-start | bytes 1572868
Sparse Core Ops, SparseCore 0:
  548.8 200.3 reduce-scatter.4
  751.6 187.9 reduce-scatter.2
